TPU v7x, 256 devices: a whole 4x4x8 slice. The times are simulated.
256 devices in a mesh: dp: 2 (over z_hi), group: 16 (over x, y), seq: 8 (over z_lo, core).
Axes of the slice: x: 4, y: 4, z: 8 (z_hi: 2, z_lo: 4; z = z_hi * 4 + z_lo), core: 2. Of those that a mesh axis runs over, the one named last changes fastest.
Arguments:
- queries: bfloat16 [2, 4096, 2560], P('dp', 'group', 'seq'), may hold values from -6 to 6
- keys: bfloat16 [2, 4096, 2560], P('dp', 'group', 'seq'), may hold values from -6 to 6
- values: bfloat16 [2, 4096, 2560], P('dp', 'group', 'seq'), may hold values from -6 to 6
- cotangent: bfloat16 [2, 4096, 2560], P('dp', 'group', 'seq'), may hold values from -18 to 18
- level_bias: float32 [3, 40], P(None, 'seq'), may hold values from -3 to 3
- off_mid: int32 [40], P('seq'), may hold values from 0 to 7
- off_far: int32 [40], P('seq'), may hold values from 0 to 63
Outputs:
- attended: bfloat16 [2, 4096, 2560], P('dp', 'group', 'seq')
- query_grad: bfloat16 [2, 4096, 2560], P('dp', 'group', 'seq')
- key_grad: bfloat16 [2, 4096, 2560], P('dp', 'group', 'seq')
- value_grad: bfloat16 [2, 4096, 2560], P('dp', 'group', 'seq')
- bias_grad: float32 [3, 40], replicated
All inputs are finite; a program needn't handle non-finite values.
Results may differ from a plain program's by a relative error of at most 0.04.
Values may be sent and summed in bfloat16 or wider, within the bound.
No kernel may reach another device: no remote copies, remote signals or barrier semaphores. Data moves between devices by JAX's collectives and lax.ppermute only.
A program may use at most 64 MiB of HBM per device.

v0:
```python
import math

import jax
import jax.numpy as jnp
from jax import lax
from jax.sharding import Mesh
from jax.sharding import PartitionSpec as P

HEADS = 40
R_MID = 8
R_FAR = 64
GROUP = ("group_0", "group_1")
SEQ = ("seq_0", "seq_1")
DP_GROUP_SEQ = ("dp", "group_0", "group_1", "seq_0", "seq_1")


def sent_together(arrays, axis, dim, along):
    widths = [a.shape[along] for a in arrays]
    both = jnp.concatenate(arrays, axis=along)
    filled = lax.all_gather(both, axis, axis=dim, tiled=True)
    return tuple(jnp.split(filled, [sum(widths[:k]) for k in range(1, len(widths))], axis=along))


def one_axis_at_a_time(array, axes):
    for axis in axes:
        array = lax.psum(array, axis)
    return array


def split_up(array, dim, count):
    before, after = (array.shape[:dim], array.shape[dim + 1 :])
    return jnp.moveaxis(array.reshape(*before, count, -1, *after), dim, 0)


def sent_and_summed(array, axis, dim):
    count = lax.axis_size(axis)
    pieces = lax.all_to_all(split_up(array, dim, count), axis, 0, 0, tiled=True)
    return jnp.sum(pieces.astype(jnp.float32), axis=0)


def side_by_side(arrays, axis, dim, along):
    ends, at = ([], 0)
    for a in arrays[:-1]:
        at += a.shape[along]
        ends.append(at)
    both = jnp.concatenate(arrays, axis=along)
    return tuple(jnp.split(sent_and_summed(both, axis, dim), ends, axis=along))


def select_rows(source, stride, offsets):
    count = source.shape[0] // stride
    shaped = source.reshape((count, stride) + source.shape[1:])
    picker = offsets.reshape((1, 1, -1) + (1,) * (source.ndim - 2))
    picker = jnp.broadcast_to(picker, (count, 1) + source.shape[1:])
    return jnp.take_along_axis(shaped, picker, axis=1)[:, 0]


def place_rows(source, stride, offsets, filler):
    heads = source.shape[1]
    marked = jnp.arange(stride, dtype=jnp.int32)[:, None] == offsets[None, :]
    marked = marked.reshape((1, stride, heads) + (1,) * (source.ndim - 2))
    spread = jnp.where(marked, source[:, None], jnp.asarray(filler, source.dtype))
    return spread.reshape((source.shape[0] * stride,) + source.shape[1:])


def forward_level(queries, keys, values, visible, scaling):
    scores = jnp.einsum("qhe,khe->hqk", queries, keys, preferred_element_type=jnp.float32) * scaling
    scores = jnp.where(visible[None], scores, -jnp.inf)
    highest = jnp.max(scores, axis=2, keepdims=True)
    log_sum = highest + jnp.log(jnp.sum(jnp.exp(scores - highest), axis=2, keepdims=True))
    weights = jnp.exp(scores - log_sum).astype(jnp.bfloat16)
    outputs = jnp.einsum("hqk,khe->qhe", weights, values, preferred_element_type=jnp.float32)
    return (log_sum[:, :, 0].T, outputs)


def backward_level(
    queries, keys, values, cotangent, visible, log_total, row_delta, bias_row, scaling
):
    scores = jnp.einsum("qhe,khe->hqk", queries, keys, preferred_element_type=jnp.float32) * scaling
    shifted = scores + bias_row[:, None, None] - log_total.T[:, :, None]
    weight = jnp.where(visible[None], jnp.exp(jnp.where(visible[None], shifted, 0.0)), 0.0)
    inner = jnp.einsum("qhe,khe->hqk", cotangent, values, preferred_element_type=jnp.float32)
    dscore = weight * (inner - row_delta.T[:, :, None])
    dscore_low = dscore.astype(jnp.bfloat16)
    weight_low = weight.astype(jnp.bfloat16)
    query_part = jnp.einsum("hqk,khe->qhe", dscore_low, keys, preferred_element_type=jnp.float32)
    key_part = jnp.einsum("hqk,qhe->khe", dscore_low, queries, preferred_element_type=jnp.float32)
    value_part = jnp.einsum(
        "hqk,qhe->khe", weight_low, cotangent, preferred_element_type=jnp.float32
    )
    return (query_part, key_part, value_part)


def causal_forward(queries, keys, values, scaling):
    length = queries.shape[0]
    block_rows = min(128, length)
    lse_parts = []
    out_parts = []
    for first_row in range(0, length, block_rows):
        last_row = first_row + block_rows
        query_place = jnp.arange(first_row, last_row, dtype=jnp.int32)
        key_place = jnp.arange(last_row, dtype=jnp.int32)
        visible = key_place[None, :] <= query_place[:, None]
        block_lse, block_out = forward_level(
            queries[first_row:last_row], keys[:last_row], values[:last_row], visible, scaling
        )
        lse_parts.append(block_lse)
        out_parts.append(block_out)
    return (jnp.concatenate(lse_parts, 0), jnp.concatenate(out_parts, 0))


def causal_backward(queries, keys, values, cotangent, log_total, row_delta, bias_row, scaling):
    length = queries.shape[0]
    block_rows = min(128, length)
    query_parts = []
    key_total = jnp.zeros(keys.shape, jnp.float32)
    value_total = jnp.zeros(values.shape, jnp.float32)
    for first_row in range(0, length, block_rows):
        last_row = first_row + block_rows
        query_place = jnp.arange(first_row, last_row, dtype=jnp.int32)
        key_place = jnp.arange(last_row, dtype=jnp.int32)
        visible = key_place[None, :] <= query_place[:, None]
        part_q, part_k, part_v = backward_level(
            queries[first_row:last_row],
            keys[:last_row],
            values[:last_row],
            cotangent[first_row:last_row],
            visible,
            log_total[first_row:last_row],
            row_delta[first_row:last_row],
            bias_row,
            scaling,
        )
        query_parts.append(part_q)
        padding = ((0, length - last_row), (0, 0), (0, 0))
        key_total = key_total + jnp.pad(part_k, padding)
        value_total = value_total + jnp.pad(part_v, padding)
    return (jnp.concatenate(query_parts, 0), key_total, value_total)


def blocked_forward(queries, keys, values, query_start, scaling, block_rows):
    key_place = jnp.arange(keys.shape[0], dtype=jnp.int32)
    query_place = query_start + jnp.arange(0, block_rows, dtype=jnp.int32)
    visible = key_place[None, :] <= query_place[:, None]
    block_lse, block_out = forward_level(queries, keys, values, visible, scaling)
    return (block_lse, block_out)


def blocked_backward(
    queries,
    keys,
    values,
    cotangent,
    log_total,
    row_delta,
    query_start,
    bias_row,
    scaling,
    block_rows,
):
    key_place = jnp.arange(keys.shape[0], dtype=jnp.int32)
    query_place = query_start + jnp.arange(0, block_rows, dtype=jnp.int32)
    visible = key_place[None, :] <= query_place[:, None]
    part_q, part_k, part_v = backward_level(
        queries, keys, values, cotangent, visible, log_total, row_delta, bias_row, scaling
    )
    return (part_q, part_k, part_v)


def per_device(queries, keys, values, cotangent, level_bias, off_mid, off_far):
    tok_rows = queries.shape[1]
    width = queries.shape[2]
    local_heads = level_bias.shape[1]
    head_size = width // local_heads
    scaling = head_size ** (-0.5)
    shape_rows = (tok_rows, local_heads, head_size)
    query_rows = queries[0].reshape(shape_rows)
    key_rows = keys[0].reshape(shape_rows)
    value_rows = values[0].reshape(shape_rows)
    grad_rows = cotangent[0].reshape(shape_rows)
    group_place = lax.axis_index(GROUP)
    anchor = jnp.zeros((), jnp.int32)
    near_lse, near_out = causal_forward(query_rows, key_rows, value_rows, scaling)
    mid_count = tok_rows // R_MID
    mid_start = group_place * mid_count
    mid_block = min(64, mid_count)
    mid_queries = select_rows(query_rows, R_MID, off_mid)
    mid_keys = select_rows(key_rows, R_MID, off_mid)
    mid_values = select_rows(value_rows, R_MID, off_mid)
    mid_all_keys, mid_all_values = (
        lax.all_gather(mid_keys, GROUP, axis=0, tiled=True),
        lax.all_gather(mid_values, GROUP, axis=0, tiled=True),
    )
    mid_lse, mid_out = blocked_forward(
        mid_queries, mid_all_keys, mid_all_values, mid_start, scaling, mid_block
    )
    far_count = tok_rows // R_FAR
    far_start = group_place * far_count
    far_queries = select_rows(query_rows, R_FAR, off_far)
    far_keys = select_rows(key_rows, R_FAR, off_far)
    far_values = select_rows(value_rows, R_FAR, off_far)
    far_all_keys, far_all_values = sent_together((far_keys, far_values), GROUP, 0, 1)
    far_lse, far_out = blocked_forward(
        far_queries, far_all_keys, far_all_values, far_start, scaling, far_count
    )
    gate_near = near_lse + level_bias[0][None, :]
    gate_mid = place_rows(mid_lse, R_MID, off_mid, -jnp.inf) + level_bias[1][None, :]
    gate_far = place_rows(far_lse, R_FAR, off_far, -jnp.inf) + level_bias[2][None, :]
    highest = jnp.maximum(gate_near, jnp.maximum(gate_mid, gate_far))
    log_total = highest + jnp.log(
        jnp.exp(gate_near - highest) + jnp.exp(gate_mid - highest) + jnp.exp(gate_far - highest)
    )
    share_near = jnp.exp(gate_near - log_total)
    share_mid = jnp.exp(gate_mid - log_total)
    share_far = jnp.exp(gate_far - log_total)
    mid_full = place_rows(mid_out, R_MID, off_mid, 0.0)
    far_full = place_rows(far_out, R_FAR, off_far, 0.0)
    mixed = (
        share_near[..., None] * near_out
        + share_mid[..., None] * mid_full
        + share_far[..., None] * far_full
    )
    attended = mixed.astype(jnp.bfloat16)
    grad_float = grad_rows.astype(jnp.float32)
    row_delta = jnp.sum(grad_float * attended.astype(jnp.float32), axis=2)
    level_terms = jnp.stack(
        [
            jnp.sum(share_near * (jnp.sum(grad_float * near_out, axis=2) - row_delta), axis=0),
            jnp.sum(share_mid * (jnp.sum(grad_float * mid_full, axis=2) - row_delta), axis=0),
            jnp.sum(share_far * (jnp.sum(grad_float * far_full, axis=2) - row_delta), axis=0),
        ]
    )
    placed_terms = lax.dynamic_update_slice(
        jnp.zeros((3, HEADS), jnp.float32), level_terms, (anchor, lax.axis_index(SEQ) * local_heads)
    )
    bias_total = one_axis_at_a_time(placed_terms, DP_GROUP_SEQ)
    near_dq, near_dk, near_dv = causal_backward(
        query_rows, key_rows, value_rows, grad_rows, log_total, row_delta, level_bias[0], scaling
    )
    mid_grads = select_rows(grad_rows, R_MID, off_mid)
    mid_total = select_rows(log_total, R_MID, off_mid)
    mid_delta = select_rows(row_delta, R_MID, off_mid)
    mid_dq, mid_dk_terms, mid_dv_terms = blocked_backward(
        mid_queries,
        mid_all_keys,
        mid_all_values,
        mid_grads,
        mid_total,
        mid_delta,
        mid_start,
        level_bias[1],
        scaling,
        mid_block,
    )
    mid_dk, mid_dv = side_by_side(
        (mid_dk_terms.astype(jnp.bfloat16), mid_dv_terms.astype(jnp.bfloat16)), GROUP, 0, 1
    )
    far_grads = select_rows(grad_rows, R_FAR, off_far)
    far_total = select_rows(log_total, R_FAR, off_far)
    far_delta = select_rows(row_delta, R_FAR, off_far)
    far_dq, far_dk_terms, far_dv_terms = blocked_backward(
        far_queries,
        far_all_keys,
        far_all_values,
        far_grads,
        far_total,
        far_delta,
        far_start,
        level_bias[2],
        scaling,
        far_count,
    )
    far_dk, far_dv = side_by_side(
        (far_dk_terms.astype(jnp.bfloat16), far_dv_terms.astype(jnp.bfloat16)), GROUP, 0, 1
    )
    query_grad = scaling * (
        near_dq + place_rows(mid_dq, R_MID, off_mid, 0.0) + place_rows(far_dq, R_FAR, off_far, 0.0)
    )
    key_grad = scaling * (
        near_dk + place_rows(mid_dk, R_MID, off_mid, 0.0) + place_rows(far_dk, R_FAR, off_far, 0.0)
    )
    value_grad = (
        near_dv + place_rows(mid_dv, R_MID, off_mid, 0.0) + place_rows(far_dv, R_FAR, off_far, 0.0)
    )
    bias_grad = bias_total / math.sqrt(lax.axis_size("dp") * lax.axis_size(GROUP) * tok_rows)
    out_shape = (1, tok_rows, width)
    return (
        attended.reshape(out_shape),
        query_grad.astype(jnp.bfloat16).reshape(out_shape),
        key_grad.astype(jnp.bfloat16).reshape(out_shape),
        value_grad.astype(jnp.bfloat16).reshape(out_shape),
        bias_grad,
    )


def solution(mesh):
    finer = Mesh(
        mesh.devices.reshape(mesh.shape["dp"], 4, 4, 4, 2),
        ("dp", "group_0", "group_1", "seq_0", "seq_1"),
    )
    in_specs = (
        P("dp", GROUP, SEQ),
        P("dp", GROUP, SEQ),
        P("dp", GROUP, SEQ),
        P("dp", GROUP, SEQ),
        P(None, SEQ),
        P(SEQ),
        P(SEQ),
    )
    out_specs = (
        P("dp", GROUP, SEQ),
        P("dp", GROUP, SEQ),
        P("dp", GROUP, SEQ),
        P("dp", GROUP, SEQ),
        P(),
    )
    return jax.shard_map(
        per_device, mesh=finer, in_specs=in_specs, out_specs=out_specs, check_vma=False
    )
```

profile of v0, /device:TPU:1, one launch (start us, length us, event | category | flops | bytes accessed | tf_op | source)
XLA Modules:
  0.0 703.9 jit_solution(6368570354909001349)
XLA Ops:
  3.4 1.1 reshape_reshape_squeeze.26
  4.5 1.1 copy.273
  5.6 1.2 reshape_reshape_squeeze.27
  10.2 13.7 %gather_fusion.2 = bf16[1280]{0:T(1024)(128)(2,1)S(1)} fusion(bf16[4,64,5,64]{1,0,3,2:T(4,128)(2,1)S(1)} %reshape_reshape_squeeze.26, s32[1280]{0:T(1024)S(1)} %reshape.1163), kind=kCustom, calls=%fused_computation.1.clone | custom fusion | bytes 25600 | tf_op jit(solution)/shard_map/jit(take_along_axis)/gather | solution.py:55
  23.9 13.7 %gather_fusion.3 = bf16[1280]{0:T(1024)(128)(2,1)S(1)} fusion(bf16[4,64,5,64]{1,0,3,2:T(4,128)(2,1)S(1)} %reshape_reshape_squeeze.27, s32[1280]{0:T(1024)S(1)} %reshape.1163), kind=kCustom, calls=%fused_computation.7.clone | custom fusion | bytes 25600 | tf_op jit(solution)/shard_map/jit(take_along_axis)/gather | solution.py:55
  37.7 13.7 %gather_fusion.4 = bf16[1280]{0:T(1024)(128)(2,1)S(1)} fusion(bf16[4,64,5,64]{1,0,3,2:T(4,128)(2,1)S(1)} %reshape_reshape_squeeze.28, s32[1280]{0:T(1024)S(1)} %reshape.1163), kind=kCustom, calls=%fused_computation.8.clone | custom fusion | bytes 25600 | tf_op jit(solution)/shard_map/jit(take_along_axis)/gather | solution.py:55
  51.5 13.7 %gather_fusion.10 = bf16[1280]{0:T(1024)(128)(2,1)S(1)} fusion(bf16[4,64,5,64]{1,0,3,2:T(4,128)(2,1)S(1)} %reshape_reshape_squeeze.31, s32[1280]{0:T(1024)S(1)} %reshape.1163), kind=kCustom, calls=%fused_computation.9.clone | custom fusion | bytes 25600 | tf_op jit(solution)/shard_map/jit(take_along_axis)/gather | solution.py:55
  65.9 19.7 %all_gather.10 = bf16[64,10,64]{2,1,0:T(8,128)(2,1)S(1)} all-gather(bf16[4,10,64]{2,1,0:T(8,128)(2,1)S(1)} %pad_maximum_fusion.3), channel_id=1, replica_groups=mesh['dp'=2,'group_0'=4,'group_1'=4,'seq_0'=4,'seq_1'=2] {'group_0','gro..., dimensions={0}, use_global_device_ids=true | all-gather | bytes 87040 | tf_op jit(solution)/shard_map/all_gather | solution.py:20
  87.6 105.5 %gather_fusion = bf16[10240]{0:T(1024)(128)(2,1)S(1)} fusion(bf16[32,8,5,64]{3,2,1,0:T(8,128)(2,1)S(1)} %reshape_reshape_squeeze.24, s32[10240]{0:T(1024)S(1)} %reshape.1151), kind=kCustom, calls=%fused_computation.clone | custom fusion | bytes 204800 | tf_op jit(solution)/shard_map/jit(take_along_axis)/gather | solution.py:55
  193.4 105.5 %gather_fusion.1 = bf16[10240]{0:T(1024)(128)(2,1)S(1)} fusion(bf16[32,8,5,64]{3,2,1,0:T(8,128)(2,1)S(1)} %reshape_reshape_squeeze.25, s32[10240]{0:T(1024)S(1)} %reshape.1151), kind=kCustom, calls=%fused_computation.4.clone | custom fusion | bytes 204800 | tf_op jit(solution)/shard_map/jit(take_along_axis)/gather | solution.py:55
  299.3 105.5 %gather_fusion.5 = bf16[10240]{0:T(1024)(128)(2,1)S(1)} fusion(bf16[32,8,5,64]{3,2,1,0:T(8,128)(2,1)S(1)} %reshape_reshape_squeeze.29, s32[10240]{0:T(1024)S(1)} %reshape.1151), kind=kCustom, calls=%fused_computation.5.clone | custom fusion | bytes 204800 | tf_op jit(solution)/shard_map/jit(take_along_axis)/gather | solution.py:55
  405.1 105.5 %gather_fusion.7 = bf16[10240]{0:T(1024)(128)(2,1)S(1)} fusion(bf16[32,8,5,64]{3,2,1,0:T(8,128)(2,1)S(1)} %reshape_reshape_squeeze.30, s32[10240]{0:T(1024)S(1)} %reshape.1151), kind=kCustom, calls=%fused_computation.6.clone | custom fusion | bytes 204800 | tf_op jit(solution)/shard_map/jit(take_along_axis)/gather | solution.py:55
  511.5 18.2 %all-gather = bf16[512,1,5,64]{3,0,2,1:T(8,128)(2,1)S(1)} all-gather(bf16[32,1,5,64]{3,0,2,1:T(8,128)(2,1)S(1)} %copy.275), channel_id=2, replica_groups=mesh['dp'=2,'group_0'=4,'group_1'=4,'seq_0'=4,'seq_1'=2] {'group_0','gro..., dimensions={0}, use_global_device_ids=true | all-gather | bytes 348160 | tf_op jit(solution)/shard_map/all_gather | solution.py:191
  534.3 1.1 broadcast_in_dim.438
  535.5 17.0 %all-gather.1 = bf16[512,1,5,64]{3,0,2,1:T(8,128)(2,1)S(1)} all-gather(bf16[32,1,5,64]{3,0,2,1:T(8,128)(2,1)S(1)} %copy.286), channel_id=3, replica_groups=mesh['dp'=2,'group_0'=4,'group_1'=4,'seq_0'=4,'seq_1'=2] {'group_0','gro..., dimensions={0}, use_global_device_ids=true | all-gather | bytes 348160 | tf_op jit(solution)/shard_map/all_gather | solution.py:192
  552.5 0.9 convolution_bitcast_fusion.5
  554.1 0.9 broadcast_bitcast_fusion.2
  555.0 2.0 copy.296
  557.0 1.9 fusion.37
  559.0 1.8 fusion.49
  561.1 1.5 fusion.35
  562.6 1.6 multiply_reduce_fusion.2
  565.2 0.8 copy.302
  567.3 0.9 gather_fusion.9
  568.4 0.9 gather_fusion.11
  570.2 0.9 fusion.18
  571.1 1.1 fusion.20
  573.5 1.7 copy.328
  575.2 1.6 copy.392
  576.8 1.7 reshape.1221
  578.5 4.4 all-to-all-start.1
  585.4 2.2 gather_fusion.6
  587.8 2.7 gather_fusion.8
  591.9 1.2 fusion.8
  593.2 1.3 fusion.16
  594.5 1.2 fusion.7
  595.7 0.9 convolution_bitcast_fusion.4
  597.0 0.9 convolution_bitcast_fusion.3
  597.9 0.8 fusion.121
  598.8 1.1 broadcast_in_dim.434
  601.8 1.7 reshape.1223
  608.2 0.9 copy.290
  609.2 0.9 copy.294
  610.1 1.0 broadcast_in_dim.428.clone
  611.1 1.0 broadcast_in_dim.429
  612.1 1.8 copy.283
  614.7 1.3 broadcast_in_dim.431
  616.0 1.1 copy.293
  617.1 1.3 broadcast_in_dim.426
  618.5 1.7 copy.289
  620.2 2.3 fusion.31
  622.8 9.2 %psum.35 = f32[3,40]{1,0:T(4,128)S(1)} all-reduce(f32[3,40]{1,0:T(4,128)S(1)} %dynamic_update_slice.3), channel_id=1, replica_groups=mesh['dp'=2,'group_0'=4,'group_1'=4,'seq_0'=4,'seq_1'=2] {'dp'}, use_global_device_ids=true, to_apply=%region_17.22 | all-reduce | flops 120 | bytes 960 | tf_op jit(solution)/shard_map/psum | solution.py:26
  632.0 8.5 %psum.36 = f32[3,40]{1,0:T(4,128)S(1)} all-reduce(f32[3,40]{1,0:T(4,128)S(1)} %psum.35), channel_id=1, replica_groups=mesh['dp'=2,'group_0'=4,'group_1'=4,'seq_0'=4,'seq_1'=2] {'group_0'}, use_global_device_ids=true, to_apply=%region_18.23 | all-reduce | flops 120 | bytes 960 | tf_op jit(solution)/shard_map/psum | solution.py:26
  640.5 8.7 %psum.37 = f32[3,40]{1,0:T(4,128)S(1)} all-reduce(f32[3,40]{1,0:T(4,128)S(1)} %psum.36), channel_id=1, replica_groups=mesh['dp'=2,'group_0'=4,'group_1'=4,'seq_0'=4,'seq_1'=2] {'group_1'}, use_global_device_ids=true, to_apply=%region_19.24 | all-reduce | flops 120 | bytes 960 | tf_op jit(solution)/shard_map/psum | solution.py:26
  649.2 9.4 %psum.38 = f32[3,40]{1,0:T(4,128)S(1)} all-reduce(f32[3,40]{1,0:T(4,128)S(1)} %psum.37), channel_id=1, replica_groups=mesh['dp'=2,'group_0'=4,'group_1'=4,'seq_0'=4,'seq_1'=2] {'seq_0'}, use_global_device_ids=true, to_apply=%region_20.25 | all-reduce | flops 120 | bytes 960 | tf_op jit(solution)/shard_map/psum | solution.py:26
  658.6 26.1 %psum.39 = f32[3,40]{1,0:T(4,128)S(1)} all-reduce(f32[3,40]{1,0:T(4,128)S(1)} %psum.38), channel_id=1, replica_groups=mesh['dp'=2,'group_0'=4,'group_1'=4,'seq_0'=4,'seq_1'=2] {'seq_1'}, use_global_device_ids=true, to_apply=%region_21.26 | all-reduce | flops 120 | bytes 960 | tf_op jit(solution)/shard_map/psum | solution.py:26
  684.7 3.9 all-to-all-start
  690.8 1.0 convolution_bitcast_fusion.2
  691.8 1.0 reshape.1222
  693.5 1.1 broadcast_in_dim.461
  695.5 4.1 all-to-all-done
  699.7 0.8 reshape.1224
  701.9 1.0 fusion.14
  703.0 0.9 fusion.15
  (368 shorter events, 37.5 us)
Async XLA Ops:
  0.6 6.1 copy-start
  0.6 6.3 copy-start.6
  0.7 6.7 copy-start.4
  1.4 63.8 %copy-start.81 = (s32[5]{0:T(128)}, s32[5]{0:T(128)S(1)}, u32[]{:S(2)}) copy-start(s32[5]{0:T(128)S(1)} %broadcast_add_fusion) | copy-start | bytes 64
  2.0 63.2 %copy-start.83 = (pred[5]{0:T(512)(128)(4,1)}, pred[5]{0:T(512)(128)(4,1)S(1)}, u32[]{:S(2)}) copy-start(pred[5]{0:T(512)(128)(4,1)S(1)} %broadcast_compare_fusion) | copy-start | bytes 19
  2.7 508.0 %copy-start.75 = (s32[5]{0:T(128)}, s32[5]{0:T(128)S(1)}, u32[]{:S(2)}) copy-start(s32[5]{0:T(128)S(1)} %broadcast_add_fusion.1) | copy-start | bytes 64
  3.4 507.4 %copy-start.77 = (pred[5]{0:T(512)(128)(4,1)}, pred[5]{0:T(512)(128)(4,1)S(1)}, u32[]{:S(2)}) copy-start(pred[5]{0:T(512)(128)(4,1)S(1)} %broadcast_compare_fusion.1) | copy-start | bytes 19
  5.6 2.1 copy-start.11
  7.7 523.8 %copy-start.20 = (bf16[1,128,320]{1,2,0:T(8,128)(2,1)}, bf16[1,128,320]{1,2,0:T(8,128)(2,1)S(1)}, u32[]{:S(2)}) copy-start(bf16[1,128,320]{1,2,0:T(8,128)(2,1)S(1)} %get-tuple-element.51) | copy-start | bytes 245764
  7.8 588.9 %copy-start.32 = (pred[128,128]{0,1:T(8,128)(4,1)}, pred[128,128]{0,1:T(8,128)(4,1)S(1)}, u32[]{:S(2)}) copy-start(pred[128,128]{0,1:T(8,128)(4,1)S(1)} %iota_compare_fusion.2) | copy-start | bytes 49156
  7.8 523.7 %copy-start.22 = (bf16[1,128,320]{1,2,0:T(8,128)(2,1)}, bf16[1,128,320]{1,2,0:T(8,128)(2,1)S(1)}, u32[]{:S(2)}) copy-start(bf16[1,128,320]{1,2,0:T(8,128)(2,1)S(1)} %slice.66) | copy-start | bytes 245764
  7.9 2.3 copy-start.88
  9.3 523.6 %copy-start.40 = (pred[256,5]{0,1:T(8,128)(4,1)}, pred[256,5]{0,1:T(8,128)(4,1)S(1)}, u32[]{:S(2)}) copy-start(pred[256,5]{0,1:T(8,128)(4,1)S(1)} %broadcast_in_dim.420) | copy-start | bytes 3844
  65.9 21.4 %copy-start.64 = (bf16[4,5,64]{2,1,0:T(8,128)(2,1)}, bf16[4,5,64]{2,1,0:T(8,128)(2,1)S(1)}, u32[]{:S(2)}) copy-start(bf16[4,5,64]{2,1,0:T(8,128)(2,1)S(1)} %get-tuple-element.78) | copy-start | bytes 7684
  86.4 447.1 %copy-start.99 = (pred[4,64]{1,0:T(4,128)(4,1)}, pred[4,64]{1,0:T(4,128)(4,1)S(1)}, u32[]{:S(2)}) copy-start(pred[4,64]{1,0:T(4,128)(4,1)S(1)} %iota_compare_fusion.5) | copy-start | bytes 772
  86.6 446.9 %copy-start.57 = (f32[5,4,64]{2,1,0:T(4,128)}, f32[5,4,64]{2,1,0:T(4,128)S(1)}, u32[]{:S(2)}) copy-start(f32[5,4,64]{2,1,0:T(4,128)S(1)} %get-tuple-element.82) | copy-start | bytes 15364
  86.8 446.7 %copy-start.54 = (f32[5,4]{1,0:T(8,128)}, f32[5,4]{1,0:T(8,128)S(1)}, u32[]{:S(2)}) copy-start(f32[5,4]{1,0:T(8,128)S(1)} %log_add_fusion.4) | copy-start | bytes 244
  511.5 19.0 %copy-start.28 = (bf16[32,5,64]{2,1,0:T(8,128)(2,1)}, bf16[32,5,64]{2,1,0:T(8,128)(2,1)S(1)}, u32[]{:S(2)}) copy-start(bf16[32,5,64]{2,1,0:T(8,128)(2,1)S(1)} %get-tuple-element.70) | copy-start | bytes 61444
  530.8 2.1 copy-start.26
  530.8 2.8 copy-start.37
  531.5 3.9 copy-start.38
  531.8 27.2 %copy-start.1 = (f32[5,128,128]{1,2,0:T(8,128)}, f32[5,128,128]{1,2,0:T(8,128)S(1)}, u32[]{:S(2)}) copy-start(f32[5,128,128]{1,2,0:T(8,128)S(1)} %get-tuple-element.86) | copy-start | bytes 983044
  531.9 3.5 copy-start.39
  532.1 3.3 copy-start.46
  532.8 2.6 copy-start.50
  557.0 3.7 copy-start.55
  560.7 6.5 copy-start.56
  560.7 6.5 copy-start.60
  560.7 6.5 copy-start.62
  560.7 6.5 copy-start.68
  560.7 6.5 copy-start.89
  568.3 3.9 copy-start.65
  569.3 13.7 %copy-start.74 = (s32[5]{0:T(128)S(1)}, s32[5]{0:T(128)}, u32[]{:S(2)}) copy-start(s32[5]{0:T(128)} %param.20) | copy-start | bytes 64
  569.3 13.7 %copy-start.76 = (s32[5]{0:T(128)S(1)}, s32[5]{0:T(128)}, u32[]{:S(2)}) copy-start(s32[5]{0:T(128)} %copy-done.75) | copy-start | bytes 64
  569.3 14.5 %copy-start.51 = (f32[256,5]{0,1:T(8,128)S(1)}, f32[256,5]{0,1:T(8,128)}, u32[]{:S(2)}) copy-start(f32[256,5]{0,1:T(8,128)} %copy-done.50) | copy-start | bytes 15364
  569.3 15.1 %copy-start.5 = (bf16[1,256,320]{1,2,0:T(8,128)(2,1)S(1)}, bf16[1,256,320]{1,2,0:T(8,128)(2,1)}, u32[]{:S(2)}) copy-start(bf16[1,256,320]{1,2,0:T(8,128)(2,1)} %param.18) | copy-start | bytes 491524
  578.5 106.2 %all-to-all-start.1 = ((bf16[16,2,1280]{2,1,0:T(2,128)(2,1)}), bf16[16,2,1280]{2,1,0:T(2,128)(2,1)}, u32[]{:S(2)}, u32[]{:S(2)}) async-start(bf16[16,2,1280]{2,1,0:T(2,128)(2,1)} %reshape.1221), calls=%async_computation.1 | async-start | bytes 163840 | tf_op jit(solution)/shard_map/all_to_all | solution.py:37
  587.7 2.8 copy-start.78
  593.1 3.4 copy-start.36
  593.1 3.4 copy-start.86
  593.1 3.5 copy-start.2
  593.1 3.5 copy-start.29
  593.2 3.5 copy-start.44
  593.2 3.5 copy-start.69
  593.2 3.5 copy-start.92
  593.2 3.5 copy-start.95
  594.5 2.5 copy-start.21
  594.5 3.4 copy-start.23
  596.7 3.2 copy-start.19
  610.1 3.8 copy-start.10
  612.1 8.1 %copy-start.8 = (f32[1,256,320]{2,1,0:T(8,128)S(1)}, f32[1,256,320]{2,1,0:T(8,128)}, u32[]{:S(2)}) copy-start(f32[1,256,320]{2,1,0:T(8,128)} %copy.290) | copy-start | bytes 983044
  612.1 8.1 %copy-start.9 = (f32[1,256,320]{2,1,0:T(8,128)S(1)}, f32[1,256,320]{2,1,0:T(8,128)}, u32[]{:S(2)}) copy-start(f32[1,256,320]{2,1,0:T(8,128)} %copy.294) | copy-start | bytes 983044
  612.1 8.1 %copy-start.17 = (f32[1,128,320]{2,1,0:T(8,128)S(1)}, f32[1,128,320]{2,1,0:T(8,128)}, u32[]{:S(2)}) copy-start(f32[1,128,320]{2,1,0:T(8,128)} %copy.299) | copy-start | bytes 491524
  620.2 2.3 copy-start.96
  620.2 2.3 copy-start.97
  620.2 2.3 copy-start.98
  622.5 66.7 %copy-start.16 = (bf16[1,256,320]{2,1,0:T(8,128)(2,1)S(1)}, bf16[1,256,320]{2,1,0:T(8,128)(2,1)}, u32[]{:S(2)}) copy-start(bf16[1,256,320]{2,1,0:T(8,128)(2,1)} %get-tuple-element.46) | copy-start | bytes 491524
  622.5 67.5 %copy-start.15 = (bf16[1,256,320]{2,1,0:T(8,128)(2,1)S(1)}, bf16[1,256,320]{2,1,0:T(8,128)(2,1)}, u32[]{:S(2)}) copy-start(bf16[1,256,320]{2,1,0:T(8,128)(2,1)} %get-tuple-element.45) | copy-start | bytes 491524
  622.5 68.3 %copy-start.3 = (f32[5,128,128]{1,2,0:T(8,128)S(1)}, f32[5,128,128]{1,2,0:T(8,128)}, u32[]{:S(2)}) copy-start(f32[5,128,128]{1,2,0:T(8,128)} %copy-done.1) | copy-start | bytes 983044
  622.5 68.3 %copy-start.33 = (pred[128,128]{0,1:T(8,128)(4,1)S(1)}, pred[128,128]{0,1:T(8,128)(4,1)}, u32[]{:S(2)}) copy-start(pred[128,128]{0,1:T(8,128)(4,1)} %copy-done.32) | copy-start | bytes 49156
  622.5 68.3 %copy-start.45 = (bf16[1,128,320]{1,2,0:T(8,128)(2,1)S(1)}, bf16[1,128,320]{1,2,0:T(8,128)(2,1)}, u32[]{:S(2)}) copy-start(bf16[1,128,320]{1,2,0:T(8,128)(2,1)} %get-tuple-element.49) | copy-start | bytes 245764
  622.5 68.3 %copy-start.71 = (f32[5]{0:T(128)S(1)}, f32[5]{0:T(128)}, u32[]{:S(2)}) copy-start(f32[5]{0:T(128)} %copy-done.67) | copy-start | bytes 64
  622.5 68.3 %copy-start.93 = (f32[5,128]{1,0:T(8,128)S(1)}, f32[5,128]{1,0:T(8,128)}, u32[]{:S(2)}) copy-start(f32[5,128]{1,0:T(8,128)} %get-tuple-element.88) | copy-start | bytes 7684
  684.7 14.9 %all-to-all-start = ((bf16[16,2,10240]{2,1,0:T(2,128)(2,1)}), bf16[16,2,10240]{2,1,0:T(2,128)(2,1)S(1)}, u32[]{:S(2)}, u32[]{:S(2)}) async-start(bf16[16,2,10240]{2,1,0:T(2,128)(2,1)} %reshape.1223), calls=%async_computation | async-start | bytes 1310720 | tf_op jit(solution)/shard_map/all_to_all | solution.py:37
  (40 other events, 55.8 us)
where the time goes:
time: 705 us; the launch traced here: 704 us
  local copies, waits for them, and re-layouts  537 us (76%)
  blocking collectives  117 us (17%)
  matrix products  18.4 us (3%)
  other arithmetic  17 us (2%)
  starting transfers between devices  8.28 us (1%)
    gather x29, local copies, waits for them, and re-layouts, select_rows(): return jnp.take_along_axis(shaped, picker, axis=1)[:, 0]  485 us
    psum x5, blocking collectives, one_axis_at_a_time(): array = lax.psum(array, axis)  61.9 us
    broadcast_in_dim x38, local copies, waits for them, and re-layouts, place_rows(): jnp.where(marked, source[:, None], jnp.asarray(filler, source.dtype))  20.4 us
    all_gather x1, blocking collectives, sent_together(): filled = lax.all_gather(both, axis, axis=dim, tiled=True)  19.7 us
    all_gather x1, blocking collectives, per_device(): lax.all_gather(mid_keys, GROUP, axis=0, tiled=True)  18.2 us
    all_gather x1, blocking collectives, per_device(): lax.all_gather(mid_values, GROUP, axis=0, tiled=True)  17 us
  transfers between devices with their start and end apart: 2, of which 1 were waited for; matrix products, arithmetic and copies ran while one was open for 6% of the time, Pallas kernels for 0%

commit v1 on v0

v1 whole, which is shorter than its diff:
```python
import functools
import math

import jax
import jax.numpy as jnp
from jax import lax
from jax.experimental import pallas as pl
from jax.experimental.pallas import tpu as pltpu
from jax.sharding import Mesh
from jax.sharding import PartitionSpec as P

HD = 64
R_MID = 8
R_FAR = 64
GROUP = ("group_0", "group_1")
SEQ = ("seq_0", "seq_1")
DP_SEQ = ("dp", "seq_0", "seq_1")

ROWS = 40
COLS = 384
MID_ROWS = 32
FAR_ROWS = 4
SUM_ROW = MID_ROWS + FAR_ROWS
STRIDE = 3
STAT = 5 * HD
BACK_STAT = 4 * HD
HIDDEN = -1e30
FAR_AWAY = 1 << 20

BF16 = jnp.bfloat16
F32 = jnp.float32


def dot(left, right, left_dim=1, right_dim=0):
    return lax.dot_general(
        left, right, (((left_dim,), (right_dim,)), ((), ())), preferred_element_type=F32
    )


def three_parts(x):
    high = x.astype(BF16).astype(F32)
    middle = (x - high).astype(BF16).astype(F32)
    return high, middle, x - high - middle


def whole_sum(x):
    return jnp.sum(jnp.sum(x, axis=0, keepdims=True), axis=1, keepdims=True)


def stacked(parts, count, width):
    row = lax.broadcasted_iota(jnp.int32, (count, width), 0)
    block = jnp.zeros((count, width), F32)
    for n, part in enumerate(parts):
        block = jnp.where(row == n, part, block)
    return block


def row_places(place, mid, far):
    nested = lax.rem(far, R_MID) == mid
    in_mid = place < MID_ROWS
    in_far = jnp.logical_and(place >= MID_ROWS, place < SUM_ROW)
    in_far = jnp.logical_and(in_far, jnp.logical_not(nested))
    at = jnp.where(in_mid, place * R_MID + mid, (place - MID_ROWS) * R_FAR + far)
    return at, in_mid, in_far, nested


def picker(tok, mid, far):
    place = lax.broadcasted_iota(jnp.int32, (ROWS, tok), 0)
    token = lax.broadcasted_iota(jnp.int32, (ROWS, tok), 1)
    at, in_mid, in_far, _ = row_places(place, mid, far)
    hit = jnp.logical_and(jnp.logical_or(in_mid, in_far), at == token)
    return jnp.where(hit, 1.0, 0.0).astype(BF16)


def dilated(tok, mid, far):
    token = lax.broadcasted_iota(jnp.int32, (1, tok), 1)
    in_mid = jnp.bitwise_and(token, R_MID - 1) == mid
    in_far = jnp.bitwise_and(token, R_FAR - 1) == far
    return jnp.logical_or(in_mid, in_far)


def causal(tok):
    key_at = lax.broadcasted_iota(jnp.int32, (tok, tok), 0)
    query_at = lax.broadcasted_iota(jnp.int32, (tok, tok), 1)
    return key_at <= query_at


def near_forward_kernel(
    mid_ref, far_ref, q_ref, k_ref, v_ref, c_ref, send_ref, stat_ref, att_ref
):
    tok = q_ref.shape[2]
    heads = q_ref.shape[1] // HD
    scale = HD**-0.5
    visible = causal(tok)
    place = lax.broadcasted_iota(jnp.int32, (ROWS, HD), 0)
    lane = lax.broadcasted_iota(jnp.int32, (ROWS, HD), 1)
    lses, deltas = [], []
    for h in range(heads):
        mid, far = mid_ref[h], far_ref[h]
        own = slice(h * HD, (h + 1) * HD)
        q, k, v, c = (ref[0, own, :] for ref in (q_ref, k_ref, v_ref, c_ref))
        s = jnp.where(visible, dot(k, q, 0, 0) * scale, HIDDEN)
        top = jnp.max(s, axis=0, keepdims=True)
        p = jnp.exp(s - top)
        size = jnp.sum(p, axis=0, keepdims=True)
        lse = top + jnp.log(size)
        out = dot(v, p.astype(BF16)) * (1.0 / size)
        out_low = out.astype(BF16)
        att_ref[own, :] = out_low
        c32 = c.astype(F32)
        out_round = out_low.astype(F32)
        lses.append(lse)
        deltas.append(jnp.sum(c32 * out_round, axis=0, keepdims=True))
        rest = jnp.sum(c32 * (out - out_round), axis=0, keepdims=True)
        rest = jnp.where(dilated(tok, mid, far), 0.0, rest)
        rest = jnp.sum(rest, axis=1, keepdims=True)
        stats = stacked(three_parts(lse), HD, tok).astype(BF16)
        pieces = jnp.concatenate([q, k, v, c, out_low, stats], axis=0)
        block = dot(picker(tok, mid, far), pieces, 1, 1)
        send_ref[h * STRIDE, :, 0:STAT] = block[:, 0:STAT].astype(BF16)
        row = jnp.zeros((1, HD), F32)
        for n, part in enumerate(three_parts(rest)):
            row = jnp.where(lane[0:1] == n, part, row)
        last = jnp.where(place == SUM_ROW, row, block[:, STAT : STAT + HD])
        send_ref[h * STRIDE, :, STAT : STAT + HD] = last.astype(BF16)
    stat_ref[...] = stacked(lses + [lses[0]] * (8 - heads) + deltas, 16, tok)


def near_backward_kernel(
    mid_ref, far_ref, q_ref, k_ref, v_ref, c_ref, stat_ref, dq_ref, dk_ref, dv_ref
):
    tok = q_ref.shape[2]
    heads = q_ref.shape[1] // HD
    scale = HD**-0.5
    visible = causal(tok)
    for h in range(heads):
        own = slice(h * HD, (h + 1) * HD)
        q, k, v, c = (ref[0, own, :] for ref in (q_ref, k_ref, v_ref, c_ref))
        lse = stat_ref[h : h + 1, :]
        delta = stat_ref[8 + h : 9 + h, :]
        lse = jnp.where(dilated(tok, mid_ref[h], far_ref[h]), -HIDDEN, lse)
        s = jnp.where(visible, dot(k, q, 0, 0) * scale, HIDDEN)
        weight = jnp.exp(s - lse)
        dscore = (weight * (dot(v, c, 0, 0) - delta)).astype(BF16)
        weight = weight.astype(BF16)
        dq_ref[own, :] = dot(k, dscore)
        dk_ref[own, :] = dot(q, dscore, 1, 1)
        dv_ref[own, :] = dot(c, weight, 1, 1)


def far_kernel(
    mid_ref, far_ref, bias_ref, x_ref, y_ref, turned_ref, one_ref, two_ref, dk_ref, dv_ref
):
    total_rows = x_ref.shape[0]
    heads = mid_ref.shape[0]
    scale = HD**-0.5
    head = jnp.minimum(lax.axis_index(GROUP) // STRIDE, heads - 1)
    column = lax.axis_index(SEQ) * heads + head
    mid, far = mid_ref[head], far_ref[head]
    tok = MID_ROWS * R_MID
    b0, b1, b2 = bias_ref[0, head], bias_ref[1, head], bias_ref[2, head]
    e1 = jnp.exp(jnp.full((1, 1), b1, F32))
    e2 = jnp.exp(jnp.full((1, 1), b2, F32))
    per = 128

    def codes(row):
        slab = jnp.right_shift(row * 1639, 16)
        place = row - slab * ROWS
        at, in_mid, in_far, nested = row_places(place, mid, far)
        at = at + slab * tok
        also = jnp.logical_and(in_mid, jnp.bitwise_and(at, R_FAR - 1) == far)
        in_far = jnp.logical_or(in_far, jnp.logical_and(also, nested))
        return at, in_mid, in_far, place

    key_at, key_mid, key_far, _ = codes(lax.broadcasted_iota(jnp.int32, (total_rows, per), 0))
    one_ref[...] = jnp.where(key_mid, key_at, FAR_AWAY)
    two_ref[...] = jnp.where(key_far, key_at, FAR_AWAY)
    dk_ref[...] = jnp.zeros_like(dk_ref)
    dv_ref[...] = jnp.zeros_like(dv_ref)
    zero = jnp.zeros((1, 1), F32)
    sums = [zero, zero, zero]
    for first in range(0, total_rows, per):
        last = first + per
        turned_ref[:, first:last] = x_ref[first:last, :].T
        q = x_ref[first:last, 0:HD]
        k = x_ref[0:last, HD : 2 * HD]
        v = x_ref[0:last, 2 * HD : 3 * HD]
        c = x_ref[first:last, 3 * HD : 4 * HD]
        c_turned = turned_ref[3 * HD : 4 * HD, first:last].astype(F32)
        near = turned_ref[4 * HD : 5 * HD, first:last].astype(F32)
        stat = turned_ref[STAT : STAT + 16, first:last].astype(F32)
        row_at, row_mid, row_far, place = codes(
            lax.broadcasted_iota(jnp.int32, (1, per), 1) + first
        )
        row_one = jnp.where(row_mid, row_at, -1)
        row_two = jnp.where(row_far, row_at, -1)
        three = stat[0:1] + stat[1:2] + stat[2:3]
        sums[0] = sums[0] + jnp.where(place == SUM_ROW, three, 0.0)
        gate = jnp.where(place == SUM_ROW, 0.0, three) + b0
        one = one_ref[0:last, :] <= row_one
        two = two_ref[0:last, :] <= row_two
        factor = jnp.where(one, e1, 0.0) + jnp.where(two, e2, 0.0)
        s = jnp.where(jnp.logical_or(one, two), dot(k, q, 1, 1) * scale, HIDDEN)
        top = jnp.maximum(jnp.max(s, axis=0, keepdims=True), gate)
        plain = jnp.exp(s - top)
        weight = plain * factor
        share = jnp.exp(gate - top)
        size = jnp.sum(weight, axis=0, keepdims=True) + share
        inverse = 1.0 / size
        total = top + jnp.log(size)
        out = dot(turned_ref[2 * HD : 3 * HD, 0:last], weight.astype(BF16))
        att = ((out + share * near) * inverse).astype(BF16).astype(F32)
        delta = jnp.sum(c_turned * att, axis=0, keepdims=True)
        near_delta = jnp.sum(c_turned * near, axis=0, keepdims=True)
        sums[0] = sums[0] + share * inverse * (near_delta - delta)
        slope = (dot(v, c, 1, 1) - delta) * inverse
        raw = plain * slope
        sums[1] = sums[1] + jnp.sum(jnp.where(one, raw, 0.0), axis=0, keepdims=True) * e1
        sums[2] = sums[2] + jnp.sum(jnp.where(two, raw, 0.0), axis=0, keepdims=True) * e2
        dscore = (raw * factor).astype(BF16)
        weight_low = (weight * inverse).astype(BF16)
        dk_ref[0:last, :] += dot(dscore, q)
        dv_ref[0:last, :] += dot(weight_low, c)
        dq = dot(turned_ref[HD : 2 * HD, 0:last], dscore)
        stats = stacked(three_parts(total) + three_parts(delta), 2 * HD, per)
        y_ref[first:last, 0 : 2 * HD] = jnp.concatenate([dq, att], axis=0).T.astype(BF16)
        y_ref[first:last, BACK_STAT : BACK_STAT + 2 * HD] = stats.T.astype(BF16)
    row = lax.broadcasted_iota(jnp.int32, (total_rows, HD), 0)
    place = row - jnp.right_shift(row * 1639, 16) * ROWS
    mine = lax.broadcasted_iota(jnp.int32, (total_rows, HD), 1) == column
    dk, dv = dk_ref[...], dv_ref[...]
    sums = [three_parts(jnp.sum(part, axis=1, keepdims=True)) for part in sums]
    for n in range(2):
        here = jnp.logical_and(mine, place == SUM_ROW + n)
        dk = jnp.where(here, sums[0][n], dk)
        dv = jnp.where(here, sums[1][n], dv)
        here = jnp.logical_and(mine, place == SUM_ROW + 2 + n)
        dk = jnp.where(here, sums[2][n], dk)
    y_ref[:, 2 * HD : 3 * HD] = dk.astype(BF16)
    y_ref[:, 3 * HD : 4 * HD] = dv.astype(BF16)


def bias_kernel(heads, y_ref, out_ref):
    tile = y_ref[0, ROWS - 8 : ROWS, 2 * HD : 4 * HD].astype(F32)
    for h in range(1, heads):
        tile = tile + y_ref[h * STRIDE, ROWS - 8 : ROWS, 2 * HD : 4 * HD].astype(F32)
    out_ref[...] = jnp.broadcast_to(tile[None], out_ref.shape)


def bias_sum_kernel(factor, x_ref, out_ref):
    count = out_ref.shape[1]
    tile = jnp.sum(x_ref[...], axis=0) * factor
    first = tile[4:5] + tile[5:6]
    out_ref[0:1, :] = first[:, 0:count]
    out_ref[1:2, :] = first[:, HD : HD + count]
    out_ref[2:3, :] = (tile[6:7] + tile[7:8])[:, 0:count]


def finish_kernel(
    mid_ref,
    far_ref,
    bias_ref,
    k_ref,
    v_ref,
    send_ref,
    y_ref,
    near_ref,
    dq_ref,
    dk_ref,
    dv_ref,
    att_out,
    dq_out,
    dk_out,
    dv_out,
):
    tok = k_ref.shape[2]
    heads = k_ref.shape[1] // HD
    scale = HD**-0.5
    place = lax.broadcasted_iota(jnp.int32, (ROWS, tok), 0)
    key_at = lax.broadcasted_iota(jnp.int32, (ROWS, tok), 1)
    for h in range(heads):
        mid, far = mid_ref[h], far_ref[h]
        own = slice(h * HD, (h + 1) * HD)
        k, v = k_ref[0, own, :], v_ref[0, own, :]
        block = h * STRIDE
        q = send_ref[block, :, 0:HD]
        c = send_ref[block, :, 3 * HD : 4 * HD]
        stat = y_ref[block, :, BACK_STAT : BACK_STAT + 8].astype(F32)
        total = stat[:, 0:1] + stat[:, 1:2] + stat[:, 2:3]
        delta = stat[:, 3:4] + stat[:, 4:5] + stat[:, 5:6]
        at, in_mid, in_far, _ = row_places(place, mid, far)
        used = jnp.logical_or(in_mid, in_far)
        s = dot(q, k) * scale + (bias_ref[0, h] - total)
        weight = jnp.exp(jnp.where(jnp.logical_and(used, key_at <= at), s, HIDDEN))
        dscore = (weight * (dot(c, v) - delta)).astype(BF16)
        weight = weight.astype(BF16)
        dq = dot(dscore, k, 1, 1) + y_ref[block, :, 0:HD].astype(F32)
        rest = y_ref[block, :, HD : 4 * HD]
        pick = jnp.where(jnp.logical_and(used, key_at == at), 1.0, 0.0).astype(BF16)
        dq = dot((dq * scale).astype(BF16), pick, 0, 0).astype(BF16)
        rest = dot(rest, pick, 0, 0)
        both = dilated(tok, mid, far)
        dq_out[0, own, :] = jnp.where(both, dq, (dq_ref[own, :] * scale).astype(BF16))
        att_out[0, own, :] = jnp.where(both, rest[0:HD].astype(BF16), near_ref[own, :])
        dk = dk_ref[own, :] + dot(q, dscore, 0, 0) + rest[HD : 2 * HD]
        dk_out[0, own, :] = (dk * scale).astype(BF16)
        dv = dv_ref[own, :] + dot(c, weight, 0, 0) + rest[2 * HD : 3 * HD]
        dv_out[0, own, :] = dv.astype(BF16)


def per_device(queries, keys, values, cotangent, level_bias, off_mid, off_far):
    tok, width = queries.shape[1:]
    heads = level_bias.shape[1]
    peers = lax.axis_size(GROUP)
    others = lax.axis_size(DP_SEQ)
    all_heads = heads * lax.axis_size(SEQ)
    smem = pl.BlockSpec(memory_space=pltpu.SMEM)
    vmem = pl.BlockSpec(memory_space=pltpu.VMEM)
    queries, keys, values, cotangent = (
        jnp.swapaxes(a, 1, 2) for a in (queries, keys, values, cotangent)
    )
    slab = (queries, keys, values, cotangent)
    shape = jax.ShapeDtypeStruct

    def call(kernel, name, in_specs, out_shape, flops, scratch=()):
        single = not isinstance(out_shape, list)
        return pl.pallas_call(
            kernel,
            name=name,
            in_specs=in_specs,
            out_specs=vmem if single else [vmem] * len(out_shape),
            out_shape=out_shape,
            scratch_shapes=list(scratch),
            compiler_params=pltpu.CompilerParams(vmem_limit_bytes=24 << 20),
            cost_estimate=pl.CostEstimate(
                flops=flops, transcendentals=0, bytes_accessed=1 << 20
            ),
        )

    send, stats, near = call(
        near_forward_kernel,
        "near_forward",
        [smem, smem] + [vmem] * 4,
        [
            shape((peers, ROWS, COLS), BF16),
            shape((16, tok), F32),
            shape((width, tok), BF16),
        ],
        200_000_000,
    )(off_mid, off_far, *slab)
    taken = lax.all_to_all(send, GROUP, 0, 0, tiled=True)
    near_grads = call(
        near_backward_kernel,
        "near_backward",
        [smem, smem] + [vmem] * 5,
        [shape((width, tok), F32)] * 3,
        400_000_000,
    )(off_mid, off_far, *slab, stats)
    taken, near_grads = lax.optimization_barrier((taken, near_grads))
    rows = peers * ROWS
    done = call(
        far_kernel,
        "mid_far",
        [smem, smem, smem, vmem],
        shape((rows, COLS), BF16),
        200_000_000,
        [
            pltpu.VMEM((COLS, rows), BF16),
            pltpu.VMEM((rows, 128), jnp.int32),
            pltpu.VMEM((rows, 128), jnp.int32),
            pltpu.VMEM((rows, HD), F32),
            pltpu.VMEM((rows, HD), F32),
        ],
    )(off_mid, off_far, level_bias, taken.reshape(rows, COLS))
    back = lax.all_to_all(done.reshape(peers, ROWS, COLS), GROUP, 0, 0, tiled=True)
    bias = call(
        functools.partial(bias_kernel, heads),
        "bias_rows",
        [vmem],
        shape((others, 8, 128), F32),
        1_000_000,
    )(back)
    bias = lax.all_to_all(bias, DP_SEQ, 0, 0, tiled=True)
    outs = call(
        finish_kernel,
        "finish",
        [smem] * 3 + [vmem] * 8,
        [shape((1, width, tok), BF16)] * 4,
        200_000_000,
    )(off_mid, off_far, level_bias, keys, values, send, back, near, *near_grads)
    factor = 1.0 / math.sqrt(lax.axis_size("dp") * peers * tok)
    bias_grad = call(
        functools.partial(bias_sum_kernel, factor),
        "bias_sum",
        [vmem],
        shape((3, all_heads), F32),
        1_000_000,
    )(bias)
    return (*(jnp.swapaxes(a, 1, 2) for a in outs), bias_grad)


def solution(mesh):
    finer = Mesh(
        mesh.devices.reshape(mesh.shape["dp"], 4, 4, 4, 2),
        ("dp", "group_0", "group_1", "seq_0", "seq_1"),
    )
    slab = P("dp", GROUP, SEQ)
    return jax.shard_map(
        per_device,
        mesh=finer,
        in_specs=(slab, slab, slab, slab, P(None, SEQ), P(SEQ), P(SEQ)),
        out_specs=(slab, slab, slab, slab, P()),
        check_vma=False,
    )
```

time: 705 us -> 63.6 us (0.09)
  local copies, waits for them, and re-layouts: 537 us -> 5.01 us
  blocking collectives: 117 us -> 12.2 us
  matrix products: 18.4 us -> 0 us
  other arithmetic: 17 us -> 0 us
  Pallas kernels: 0 us -> 13.5 us
  starting transfers between devices: 8.28 us -> 19.4 us
  waiting for transfers between devices: 4.14 us -> 12.4 us
    gather x29 -> x0, local copies, waits for them, and re-layouts: 485 us -> none  [select_rows(): return jnp.take_along_axis(shaped, picker, axis=1)[:, 0]]
    psum x5 -> x0, blocking collectives: 61.9 us -> none  [one_axis_at_a_time(): array = lax.psum(array, axis)]
    all_gather x3 -> x0, blocking collectives: 54.9 us -> none  [the longest x1 19.7 us: sent_together(): filled = lax.all_gather(both, axis, axis=dim, tiled=True)]
    broadcast_in_dim x39 -> x0, local copies, waits for them, and re-layouts: 20.4 us -> none  [the longest x38 20.4 us: place_rows(): jnp.where(marked, source[:, None], jnp.asarray(filler, source.dtype))]
    dot_general x24 -> x0, matrix products: 18.4 us -> none  [the longest x4 4.85 us: forward_level(): jnp.einsum('hqk,khe->qhe', weights, values, preferred_element_type=jnp.fl...]
    pallas_call x0 -> x6, Pallas kernels: none -> 13.5 us  [the longest x1 3.58 us: per_device(): call(near_forward_kernel, 'near_forward', [smem, smem] + [vmem] * 4, [sha...]
    all_to_all x0 -> x1, blocking collectives: none -> 12.2 us  [per_device(): lax.all_to_all(done.reshape(peers, ROWS, COLS), GROUP, 0, 0, tiled=True)]
    all_to_all x2, starting transfers between devices: 8.28 us -> 19.4 us  [the longest x1 11.7 us: per_device(): bias = lax.all_to_all(bias, DP_SEQ, 0, 0, tiled=True)]
  transfers between devices with their start and end apart: 2 -> 2, of which waited for: 1 -> 2; matrix products, arithmetic and copies ran while one was open for 6% -> 0% of each run, Pallas kernels for 0% -> 8%
where the time goes in v1:
time: 63.6 us; the launch traced here: 63.2 us
  starting transfers between devices  19.4 us (31%)
  Pallas kernels  13.5 us (21%)
  waiting for transfers between devices  12.4 us (19%)
  blocking collectives  12.2 us (19%)
  local copies, waits for them, and re-layouts  5.01 us (8%)
  between operations  0.71 us (1%)
    all_to_all x1, blocking collectives, per_device(): lax.all_to_all(done.reshape(peers, ROWS, COLS), GROUP, 0, 0, tiled=True)  12.2 us
    all_to_all x1, starting transfers between devices, per_device(): bias = lax.all_to_all(bias, DP_SEQ, 0, 0, tiled=True)  11.7 us
    all_to_all x1, waiting for transfers between devices, per_device(): taken = lax.all_to_all(send, GROUP, 0, 0, tiled=True)  7.83 us
    all_to_all x1, starting transfers between devices, per_device(): taken = lax.all_to_all(send, GROUP, 0, 0, tiled=True)  7.71 us
    unnamed x22, local copies, waits for them, and re-layouts  5.01 us
    all_to_all x1, waiting for transfers between devices, per_device(): bias = lax.all_to_all(bias, DP_SEQ, 0, 0, tiled=True)  4.58 us
    pallas_call x1, Pallas kernels, per_device(): call(near_forward_kernel, 'near_forward', [smem, smem] + [vmem] * 4, [sha...  3.58 us
    pallas_call x1, Pallas kernels, per_device(): call(far_kernel, 'mid_far', [smem, smem, smem, vmem], shape((rows, COLS),...  3.27 us
  transfers between devices with their start and end apart: 2, of which 2 were waited for; matrix products, arithmetic and copies ran while one was open for 0% of the time, Pallas kernels for 8%

profile of v1, /device:TPU:1, one launch (start us, length us, event | category | flops | bytes accessed | tf_op | source)
XLA Modules:
  0.0 63.2 jit_solution(12233374919379753643)
XLA Ops:
  0.6 0.0 copy-start.5
  0.6 0.0 copy-start.6
  0.7 0.6 %copy-done.5 = s32[5]{0:T(128)S(1)} copy-done((s32[5]{0:T(128)S(1)}, s32[5]{0:T(128)}, u32[]{:S(2)}) %copy-start.5) | copy-done | bytes 44
  1.3 0.0 copy-done.6
  1.3 0.0 copy-start
  1.3 0.9 %copy-done = bf16[1,256,320]{1,2,0:T(8,128)(2,1)S(1)} copy-done((bf16[1,256,320]{1,2,0:T(8,128)(2,1)S(1)}, bf16[1,256,320]{1,2,0:T(8,128)(2,1)}, u32[]{:S(2)}) %copy-start) | copy-done | bytes 163864
  2.2 0.0 copy-start.2
  2.2 0.9 %copy-done.2 = bf16[1,256,320]{1,2,0:T(8,128)(2,1)S(1)} copy-done((bf16[1,256,320]{1,2,0:T(8,128)(2,1)S(1)}, bf16[1,256,320]{1,2,0:T(8,128)(2,1)}, u32[]{:S(2)}) %copy-start.2) | copy-done | bytes 163864
  3.1 0.0 copy-start.7
  3.1 0.9 %copy-done.7 = bf16[1,256,320]{1,2,0:T(8,128)(2,1)S(1)} copy-done((bf16[1,256,320]{1,2,0:T(8,128)(2,1)S(1)}, bf16[1,256,320]{1,2,0:T(8,128)(2,1)}, u32[]{:S(2)}) %copy-start.7) | copy-done | bytes 163864
  4.1 0.0 copy-start.9
  4.1 0.9 %copy-done.9 = bf16[1,256,320]{1,2,0:T(8,128)(2,1)S(1)} copy-done((bf16[1,256,320]{1,2,0:T(8,128)(2,1)S(1)}, bf16[1,256,320]{1,2,0:T(8,128)(2,1)}, u32[]{:S(2)}) %copy-start.9) | copy-done | bytes 163864
  5.0 3.6 %near_forward.1 = (bf16[16,40,384]{2,1,0:T(8,128)(2,1)}, f32[16,256]{1,0:T(8,128)S(1)}, bf16[320,256]{1,0:T(8,128)(2,1)S(1)}) custom-call(s32[5]{0:T(128)S(1)} %copy-done.5, s32[5]{0:T(128)S(1)} %copy-done.6, bf16[1,320,256]{2,1,0:T(8,128)(2,1)S(1)} %bitcast.18, bf16[1,320,256]{2,1,0:T(8,128)(2,1)S(1)} %bitcast.12, bf16[1,320,256]{2,1,0:T(8,128)(2,1)S(1)} %bitcast.15, ...), custom_call_target="tpu_custom_call" | custom-call | flops 200000000 | bytes 1048576 | tf_op jit(solution)/shard_map/near_forward/pallas_call | solution.py:340
  8.5 0.0 copy-start.1
  8.5 0.0 copy-start.3
  8.6 0.0 copy-start.8
  8.6 0.0 copy-start.10
  8.6 7.7 %all-to-all-start = ((bf16[16,40,384]{2,1,0:T(8,128)(2,1)}), bf16[16,40,384]{2,1,0:T(8,128)(2,1)S(1)}, u32[]{:S(2)}, u32[]{:S(2)}) async-start(bf16[16,40,384]{2,1,0:T(8,128)(2,1)} %get-tuple-element.19.send_ref), calls=%async_computation | async-start | bytes 983040 | tf_op jit(solution)/shard_map/all_to_all | solution.py:351
  16.3 0.0 copy-done.1
  16.3 0.0 copy-done.3
  16.3 0.0 copy-done.8
  16.3 0.0 copy-done.10
  16.3 2.2 %near_backward.1 = (f32[320,256]{1,0:T(8,128)S(1)}, f32[320,256]{1,0:T(8,128)S(1)}, f32[320,256]{1,0:T(8,128)S(1)}) custom-call(s32[5]{0:T(128)S(1)} %copy-done.5, s32[5]{0:T(128)S(1)} %copy-done.6, bf16[1,320,256]{2,1,0:T(8,128)(2,1)S(1)} %bitcast.19, bf16[1,320,256]{2,1,0:T(8,128)(2,1)S(1)} %bitcast.13, bf16[1,320,256]{2,1,0:T(8,128)(2,1)S(1)} %bitcast.16, ...), custom_call_target="tpu_custom_call" | custom-call | flops 400000000 | bytes 1048576 | tf_op jit(solution)/shard_map/near_backward/pallas_call | solution.py:352
  18.5 7.8 %all-to-all-done = bf16[16,40,384]{2,1,0:T(8,128)(2,1)S(1)} async-done(((bf16[16,40,384]{2,1,0:T(8,128)(2,1)}), bf16[16,40,384]{2,1,0:T(8,128)(2,1)S(1)}, u32[]{:S(2)}, u32[]{:S(2)}) %all-to-all-start) | async-done | bytes 491552 | tf_op jit(solution)/shard_map/all_to_all | solution.py:351
  26.3 0.0 copy-start.4
  26.3 0.7 %copy-done.4 = f32[3,5]{1,0:T(4,128)S(1)} copy-done((f32[3,5]{1,0:T(4,128)S(1)}, f32[3,5]{1,0:T(4,128)}, u32[]{:S(2)}) %copy-start.4) | copy-done | bytes 84
  27.0 3.3 %mid_far.1 = bf16[640,384]{1,0:T(8,128)(2,1)S(1)} custom-call(s32[5]{0:T(128)S(1)} %copy-done.5, s32[5]{0:T(128)S(1)} %copy-done.6, f32[3,5]{1,0:T(4,128)S(1)} %copy-done.4, bf16[640,384]{1,0:T(8,128)(2,1)S(1)} %bitcast.10), custom_call_target="tpu_custom_call" | custom-call | flops 200000000 | bytes 1048576 | tf_op jit(solution)/shard_map/mid_far/pallas_call | solution.py:361
  30.3 12.2 %all_to_all.15.y_ref = bf16[16,40,384]{2,1,0:T(8,128)(2,1)S(1)} all-to-all(bf16[16,40,384]{2,1,0:T(8,128)(2,1)S(1)} %bitcast.11), channel_id=1, replica_groups=mesh['dp'=2,'group_0'=4,'group_1'=4,'seq_0'=4,'seq_1'=2] {'group_0','gro..., dimensions={0} | all-to-all | bytes 983040 | tf_op jit(solution)/shard_map/all_to_all | solution.py:375
  42.4 0.6 bias_rows.1
  43.1 11.7 %all-to-all-start.2 = ((f32[16,8,128]{2,1,0:T(8,128)}), f32[16,8,128]{2,1,0:T(8,128)S(1)}, u32[]{:S(2)}, u32[]{:S(2)}) async-start(f32[16,8,128]{2,1,0:T(8,128)} %bias_rows.1), calls=%async_computation.2 | async-start | bytes 131072 | tf_op jit(solution)/shard_map/all_to_all | solution.py:383
  54.7 3.2 %finish.1 = (bf16[1,320,256]{2,1,0:T(8,128)(2,1)}, bf16[1,320,256]{2,1,0:T(8,128)(2,1)}, bf16[1,320,256]{2,1,0:T(8,128)(2,1)}, bf16[1,320,256]{2,1,0:T(8,128)(2,1)}) custom-call(s32[5]{0:T(128)S(1)} %copy-done.5, s32[5]{0:T(128)S(1)} %copy-done.6, f32[3,5]{1,0:T(4,128)S(1)} %copy-done.4, bf16[1,320,256]{2,1,0:T(8,128)(2,1)S(1)} %bitcast.14, ...), custom_call_target="tpu_custom_call" | custom-call | flops 200000000 | bytes 1048576 | tf_op jit(solution)/shard_map/finish/pallas_call | solution.py:384
  57.9 4.6 %all-to-all-done.2.x_ref = f32[16,8,128]{2,1,0:T(8,128)S(1)} async-done(((f32[16,8,128]{2,1,0:T(8,128)}), f32[16,8,128]{2,1,0:T(8,128)S(1)}, u32[]{:S(2)}, u32[]{:S(2)}) %all-to-all-start.2) | async-done | bytes 65568 | tf_op jit(solution)/shard_map/all_to_all | solution.py:383
  62.5 0.7 %bias_sum.1 = f32[3,40]{1,0:T(4,128)} custom-call(f32[16,8,128]{2,1,0:T(8,128)S(1)} %all-to-all-done.2.x_ref), custom_call_target="tpu_custom_call" | custom-call | flops 1000000 | bytes 1048576 | tf_op jit(solution)/shard_map/bias_sum/pallas_call | solution.py:392
Async XLA Ops:
  0.6 0.7 %copy-start.5 = (s32[5]{0:T(128)S(1)}, s32[5]{0:T(128)}, u32[]{:S(2)}) copy-start(s32[5]{0:T(128)} %mid_ref.7) | copy-start | bytes 64
  0.6 0.7 %copy-start.6 = (s32[5]{0:T(128)S(1)}, s32[5]{0:T(128)}, u32[]{:S(2)}) copy-start(s32[5]{0:T(128)} %far_ref.7) | copy-start | bytes 64
  1.3 0.9 %copy-start = (bf16[1,256,320]{1,2,0:T(8,128)(2,1)S(1)}, bf16[1,256,320]{1,2,0:T(8,128)(2,1)}, u32[]{:S(2)}) copy-start(bf16[1,256,320]{1,2,0:T(8,128)(2,1)} %param.8) | copy-start | bytes 491524
  2.2 0.9 %copy-start.2 = (bf16[1,256,320]{1,2,0:T(8,128)(2,1)S(1)}, bf16[1,256,320]{1,2,0:T(8,128)(2,1)}, u32[]{:S(2)}) copy-start(bf16[1,256,320]{1,2,0:T(8,128)(2,1)} %param.9) | copy-start | bytes 491524
  3.1 0.9 %copy-start.7 = (bf16[1,256,320]{1,2,0:T(8,128)(2,1)S(1)}, bf16[1,256,320]{1,2,0:T(8,128)(2,1)}, u32[]{:S(2)}) copy-start(bf16[1,256,320]{1,2,0:T(8,128)(2,1)} %param.7) | copy-start | bytes 491524
  4.1 0.9 %copy-start.9 = (bf16[1,256,320]{1,2,0:T(8,128)(2,1)S(1)}, bf16[1,256,320]{1,2,0:T(8,128)(2,1)}, u32[]{:S(2)}) copy-start(bf16[1,256,320]{1,2,0:T(8,128)(2,1)} %param.10) | copy-start | bytes 491524
  8.5 7.7 %copy-start.1 = (bf16[1,256,320]{1,2,0:T(8,128)(2,1)S(1)}, bf16[1,256,320]{1,2,0:T(8,128)(2,1)}, u32[]{:S(2)}) copy-start(bf16[1,256,320]{1,2,0:T(8,128)(2,1)} %param.8) | copy-start | bytes 491524
  8.5 7.7 %copy-start.3 = (bf16[1,256,320]{1,2,0:T(8,128)(2,1)S(1)}, bf16[1,256,320]{1,2,0:T(8,128)(2,1)}, u32[]{:S(2)}) copy-start(bf16[1,256,320]{1,2,0:T(8,128)(2,1)} %param.9) | copy-start | bytes 491524
  8.6 7.8 %copy-start.8 = (bf16[1,256,320]{1,2,0:T(8,128)(2,1)S(1)}, bf16[1,256,320]{1,2,0:T(8,128)(2,1)}, u32[]{:S(2)}) copy-start(bf16[1,256,320]{1,2,0:T(8,128)(2,1)} %param.7) | copy-start | bytes 491524
  8.6 7.8 %copy-start.10 = (bf16[1,256,320]{1,2,0:T(8,128)(2,1)S(1)}, bf16[1,256,320]{1,2,0:T(8,128)(2,1)}, u32[]{:S(2)}) copy-start(bf16[1,256,320]{1,2,0:T(8,128)(2,1)} %param.10) | copy-start | bytes 491524
  8.6 17.8 %all-to-all-start = ((bf16[16,40,384]{2,1,0:T(8,128)(2,1)}), bf16[16,40,384]{2,1,0:T(8,128)(2,1)S(1)}, u32[]{:S(2)}, u32[]{:S(2)}) async-start(bf16[16,40,384]{2,1,0:T(8,128)(2,1)} %get-tuple-element.19.send_ref), calls=%async_computation | async-start | bytes 983040 | tf_op jit(solution)/shard_map/all_to_all | solution.py:351
  26.3 0.7 %copy-start.4 = (f32[3,5]{1,0:T(4,128)S(1)}, f32[3,5]{1,0:T(4,128)}, u32[]{:S(2)}) copy-start(f32[3,5]{1,0:T(4,128)} %bias_ref.3) | copy-start | bytes 184
  43.1 19.4 %all-to-all-start.2 = ((f32[16,8,128]{2,1,0:T(8,128)}), f32[16,8,128]{2,1,0:T(8,128)S(1)}, u32[]{:S(2)}, u32[]{:S(2)}) async-start(f32[16,8,128]{2,1,0:T(8,128)} %bias_rows.1), calls=%async_computation.2 | async-start | bytes 131072 | tf_op jit(solution)/shard_map/all_to_all | solution.py:383
